TPU v7x, 256 devices: a whole 4x4x8 slice. The times are simulated.
256 devices in a mesh: ex: 16 (over y, x_lo, core), tp: 16 (over x_hi, z).
Axes of the slice: x: 4 (x_hi: 2, x_lo: 2; x = x_hi * 2 + x_lo), y: 4, z: 8, core: 2. Of those that a mesh axis runs over, the one named last changes fastest.
Arguments:
- samples: bfloat16 [1536, 2048], P(('ex', 'tp')), may hold values from -6 to 6
- gate_weight: bfloat16 [2048, 44], replicated, may hold values from -15 to 15
- up_weight: bfloat16 [16, 2048, 4096], P('ex', None, 'tp'), may hold values from -0.125 to 0.125
- down_weight: bfloat16 [16, 4096, 2048], P('ex', 'tp'), may hold values from -0.09375 to 0.09375
Outputs:
- task_outputs: bfloat16 [1536, 5, 2048], P(('ex', 'tp'))
All inputs are finite; a program needn't handle non-finite values.
Results may differ from a plain program's by a relative error of at most 0.0055.
Values may be sent and summed in bfloat16 or wider, within the bound.
No kernel may reach another device: no remote copies, remote signals or barrier semaphores. Data moves between devices by JAX's collectives and lax.ppermute only.
A program may use at most 128 MiB of HBM per device.

v0:
```python
import jax
import jax.numpy as jnp
import numpy as np
from jax import lax
from jax.sharding import Mesh
from jax.sharding import PartitionSpec as P

TASKS = 4
TASK_EXP = 3
SHARED = 4
EXPERTS = 16
GATES = 44
TP = ("tp_0", "tp_1")
EX_TP = ("ex", "tp_0", "tp_1")


def own_block(pieces, axes, order):
    shape = [lax.axis_size(a) for a in axes]
    pieces = pieces.reshape(*shape, *pieces.shape[1:])
    pieces = pieces.transpose(*order, *range(len(axes), pieces.ndim))
    pieces = pieces.reshape(-1, *pieces.shape[len(axes) :])
    for k in order:
        pieces = lax.psum_scatter(pieces, axes[k], scatter_dimension=0, tiled=True)
    return pieces[0]


def cut_along(shard, dim, devices):
    shape = shard.shape
    pieces = shard.reshape(*shape[:dim], devices, shape[dim] // devices, *shape[dim + 1 :])
    return jnp.moveaxis(pieces, dim, 0)


def sum_by_axis(shard, axes, order, dim):
    devices = lax.axis_size(axes)
    return own_block(cut_along(shard, dim, devices), axes, order)


def routing_table():
    per_task = TASK_EXP + SHARED
    table = np.zeros((GATES, (TASKS + 1) * EXPERTS), np.float32)
    for task_idx in range(TASKS):
        for column in range(per_task):
            if column < TASK_EXP:
                expert_idx = task_idx * TASK_EXP + column
            else:
                expert_idx = TASKS * TASK_EXP + column - TASK_EXP
            table[task_idx * per_task + column, task_idx * EXPERTS + expert_idx] = 1.0
    for expert_idx in range(EXPERTS):
        table[TASKS * per_task + expert_idx, TASKS * EXPERTS + expert_idx] = 1.0
    return jnp.asarray(table, dtype=jnp.float32)


def gate_mix(rows, gate_weight):
    logits = jnp.dot(rows, gate_weight, preferred_element_type=jnp.float32)
    per_task = TASK_EXP + SHARED
    pieces = []
    for task_idx in range(TASKS):
        pieces.append(
            jax.nn.softmax(logits[:, task_idx * per_task : (task_idx + 1) * per_task], axis=-1)
        )
    pieces.append(jax.nn.softmax(logits[:, TASKS * per_task :], axis=-1))
    probs = jnp.concatenate(pieces, axis=1)
    mixed = jnp.dot(probs, routing_table(), precision=lax.Precision.HIGHEST)
    return mixed.reshape(rows.shape[0], TASKS + 1, EXPERTS)


def on_device(samples, gate_weight, up_weight, down_weight):
    local_experts = up_weight.shape[0]
    ex_count = lax.axis_size("ex")
    tp_count = lax.axis_size(TP)
    row_dev = samples.shape[0]
    width = samples.shape[1]
    outputs = [
        jnp.maximum(
            jnp.dot(
                lax.all_gather(samples, EX_TP, axis=0, tiled=True),
                up_weight[0],
                preferred_element_type=jnp.float32,
            ),
            0.0,
        ).astype(jnp.bfloat16)
    ]
    hidden = jnp.stack(outputs, axis=1)
    partial_out = jnp.einsum(
        "rlf,lfd->rld", hidden, down_weight, preferred_element_type=jnp.float32
    )
    blocked = partial_out.reshape(ex_count, tp_count * row_dev, local_experts, width)
    summed = sum_by_axis(blocked, TP, (1, 0), 1)
    gathered = lax.all_to_all(summed, "ex", split_axis=0, concat_axis=2, tiled=True)[0]
    mixing = gate_mix(samples, gate_weight)
    result = jnp.einsum("rke,red->rkd", mixing, gathered, precision=lax.Precision.HIGHEST)
    return result.astype(jnp.bfloat16)


def solution(mesh):
    torus = Mesh(mesh.devices.reshape(mesh.shape["ex"], 2, 8), ("ex", "tp_0", "tp_1"))
    return jax.shard_map(
        on_device,
        mesh=torus,
        in_specs=(P(EX_TP, None), P(), P("ex", None, TP), P("ex", TP, None)),
        out_specs=P(EX_TP, None, None),
        check_vma=False,
    )
```

profile of v0, /device:TPU:1, one launch (start us, length us, event | category | flops | bytes accessed | tf_op | source)
XLA Modules:
  0.0 1006.1 jit_solution(12490226388472743928)
XLA Ops:
  6.5 0.0 copy-start
  6.5 0.0 all-gather.3.cloned.1.call-start
  6.5 0.7 all-gather.3.cloned.1.call-update
  7.3 0.0 copy-start.2
  7.3 0.0 reduce-scatter.3.cloned.1.call-start
  7.3 727.8 %all-gather.3.cloned.1.call-done = bf16[256,6,2048]{2,1,0:T(8,128)(2,1)} async-done(((bf16[1,6,2048]{2,1,0:T(8,128)(2,1)}), bf16[256,6,2048]{2,1,0:T(8,128)(2,1)}) %all-gather.3.cloned.1.call-update) | async-done | bytes 6291472 | tf_op jit(solution)/shard_map/all_gather | solution.py:76
  735.1 11.1 %reshape.31 = bf16[1536,2048]{1,0:T(8,128)(2,1)} reshape(bf16[256,6,2048]{2,1,0:T(8,128)(2,1)} %all-gather.3.cloned.1.call-done) | data formatting | bytes 12582912
  746.2 0.0 copy-done
  746.2 0.0 copy-done.2
  746.2 13.8 %convolution_bitcast_fusion = f32[1536,1,2048]{2,0,1:T(8,128)} fusion(bf16[1,256,2048]{2,1,0:T(8,128)(2,1)S(1)} %copy-done, bf16[1536,2048]{1,0:T(8,128)(2,1)} %reshape.31, bf16[1,2048,256]{2,1,0:T(8,128)(2,1)S(1)} %copy-done.2), kind=kOutput, calls=%fused_computation | convolution fusion | flops 3222011904 | bytes 20971520 | tf_op jit(solution)/shard_map/rlf,lfd->rld/dot_general | solution.py:84
  759.9 19.3 %reshape_reshape.3 = f32[16,16,6,1,2048]{4,3,2,1,0:T(1,128)} reshape(f32[1536,1,2048]{2,0,1:T(8,128)} %convolution_bitcast_fusion) | data formatting | bytes 25165824 | tf_op jit(solution)/shard_map/reshape;reshape | solution.py:29
  779.3 18.9 %copy.21 = f32[16,16,6,1,2048]{4,1,3,2,0:T(8,128)} copy(f32[16,16,6,1,2048]{4,3,2,0,1:T(1,128)} %bitcast.40) | data formatting | bytes 25165824 | tf_op jit(solution)/shard_map/transpose | solution.py:30
  798.1 11.2 %copy.22 = f32[8,2,16,6,1,2048]{5,2,4,3,1,0:T(8,128)} copy(f32[8,2,16,6,1,2048]{5,2,4,3,0,1:T(8,128)} %bitcast.41) | data formatting | bytes 25165824 | tf_op jit(solution)/shard_map/transpose | solution.py:20
  809.4 0.0 copy-start.3
  809.4 0.0 copy-start.4
  809.4 0.0 copy-start.7
  809.4 0.0 copy-start.6
  809.4 0.0 copy-start.5
  809.4 0.0 reduce-scatter.3.cloned.1.call-update
  809.4 0.0 copy-start.1
  809.4 0.3 reduce-scatter.5.cloned.1.call-start
  809.7 133.9 %reduce-scatter.3.cloned.1.call-done = f32[2,16,6,1,2048]{4,1,3,2,0:T(8,128)} async-done(((f32[16,16,6,1,2048]{4,1,3,2,0:T(8,128)}), f32[2,16,6,1,2048]{4,1,3,2,0:T(8,128)}) %reduce-scatter.3.cloned.1.call-update) | async-done | bytes 1572880 | tf_op jit(solution)/shard_map/reduce_scatter | solution.py:23
  943.6 0.0 reduce-scatter.5.cloned.1.call-update
  943.6 0.0 copy-done.3
  943.6 0.0 copy-done.4
  943.6 0.2 fusion.29
  943.8 0.2 slice_reduce_fusion
  944.0 0.2 slice_reduce_fusion.1
  944.2 0.2 fusion.16
  944.4 0.0 copy-done.8
  944.4 0.2 fusion.10
  944.6 0.0 copy-done.9
  944.6 0.2 convolution_add_fusion.3
  944.9 32.5 %reduce-scatter.5.cloned.1.call-done = f32[1,16,6,1,2048]{4,1,3,2,0:T(8,128)} async-done(((f32[2,16,6,1,2048]{4,1,3,2,0:T(8,128)}), f32[1,16,6,1,2048]{4,1,3,2,0:T(8,128)}) %reduce-scatter.5.cloned.1.call-update) | async-done | bytes 786448 | tf_op jit(solution)/shard_map/reduce_scatter | solution.py:23
  977.4 2.8 copy.23
  980.2 5.1 all-to-all-start
  985.3 0.2 fusion.17
  985.5 0.0 copy-done.7
  985.5 0.2 convolution_add_fusion.2
  985.7 0.0 copy-done.6
  985.7 0.2 convolution_add_fusion.1
  986.0 0.0 copy-done.5
  986.0 0.2 convolution_add_fusion
  986.2 0.1 reshape.26
  986.3 11.6 %all-to-all-done = f32[16,6,1,2048]{3,2,1,0:T(1,128)S(1)} async-done(((f32[16,6,1,2048]{3,2,1,0:T(1,128)}), f32[16,6,1,2048]{3,2,1,0:T(1,128)S(1)}, u32[]{:S(2)}, u32[]{:S(2)}) %all-to-all-start) | async-done | bytes 786464 | tf_op jit(solution)/shard_map/all_to_all | solution.py:89
  997.9 0.9 convolution_convert_fusion
  998.8 0.8 copy.25
  999.6 0.0 copy-done.1
  (2 shorter events, 0.0 us)
Async XLA Ops:
  6.5 739.7 %copy-start = (bf16[1,256,2048]{2,1,0:T(8,128)(2,1)S(1)}, bf16[1,256,2048]{2,1,0:T(8,128)(2,1)}, u32[]{:S(2)}) copy-start(bf16[1,256,2048]{2,1,0:T(8,128)(2,1)} %param.8) | copy-start | bytes 3145732
  6.5 728.6 %all-gather.3.cloned.1.call-start = ((), (), s32[]{:S(2)}) async-start(), calls=%async_computation.5 | async-start | bytes 8421376 | tf_op jit(solution)/shard_map/all_gather | solution.py:76
  7.3 738.9 %copy-start.2 = (bf16[1,2048,256]{2,1,0:T(8,128)(2,1)S(1)}, bf16[1,2048,256]{2,1,0:T(8,128)(2,1)}, u32[]{:S(2)}) copy-start(bf16[1,2048,256]{2,1,0:T(8,128)(2,1)} %param.7) | copy-start | bytes 3145732
  7.3 936.3 %reduce-scatter.3.cloned.1.call-start = ((), (), s32[]{:S(2)}) async-start(), calls=%async_computation.3 | async-start | bytes 14155776 | tf_op jit(solution)/shard_map/reduce_scatter | solution.py:23
  809.4 134.3 %copy-start.3 = (bf16[2048,44]{0,1:T(8,128)(2,1)S(1)}, bf16[2048,44]{0,1:T(8,128)(2,1)}, u32[]{:S(2)}) copy-start(bf16[2048,44]{0,1:T(8,128)(2,1)} %param.6) | copy-start | bytes 540676
  809.4 134.3 %copy-start.4 = (bf16[6,2048]{1,0:T(8,128)(2,1)S(1)}, bf16[6,2048]{1,0:T(8,128)(2,1)}, u32[]{:S(2)}) copy-start(bf16[6,2048]{1,0:T(8,128)(2,1)} %param.5) | copy-start | bytes 73732
  809.4 135.1 %copy-start.8 = (f32[7,80]{1,0:T(8,128)S(1)}, f32[7,80]{1,0:T(8,128)}, u32[]{:S(2)}) copy-start(f32[7,80]{1,0:T(8,128)} %constant.12) | copy-start | bytes 6724
  809.4 135.3 %copy-start.9 = (f32[7,80]{1,0:T(8,128)S(1)}, f32[7,80]{1,0:T(8,128)}, u32[]{:S(2)}) copy-start(f32[7,80]{1,0:T(8,128)} %constant.13) | copy-start | bytes 6724
  809.4 176.2 %copy-start.7 = (f32[7,80]{1,0:T(8,128)S(1)}, f32[7,80]{1,0:T(8,128)}, u32[]{:S(2)}) copy-start(f32[7,80]{1,0:T(8,128)} %constant.14) | copy-start | bytes 6724
  809.4 176.4 %copy-start.6 = (f32[7,80]{1,0:T(8,128)S(1)}, f32[7,80]{1,0:T(8,128)}, u32[]{:S(2)}) copy-start(f32[7,80]{1,0:T(8,128)} %constant.15) | copy-start | bytes 6724
  809.4 176.6 %copy-start.5 = (f32[16,80]{1,0:T(8,128)S(1)}, f32[16,80]{1,0:T(8,128)}, u32[]{:S(2)}) copy-start(f32[16,80]{1,0:T(8,128)} %constant.16) | copy-start | bytes 15364
  809.4 190.2 %copy-start.1 = (bf16[1,256,2048]{2,1,0:T(8,128)(2,1)S(1)}, bf16[1,256,2048]{2,1,0:T(8,128)(2,1)}, u32[]{:S(2)}) copy-start(bf16[1,256,2048]{2,1,0:T(8,128)(2,1)} %param.8) | copy-start | bytes 3145732
  809.4 167.9 %reduce-scatter.5.cloned.1.call-start = ((), (), s32[]{:S(2)}) async-start(), calls=%async_computation.4 | async-start | bytes 2359296 | tf_op jit(solution)/shard_map/reduce_scatter | solution.py:23
  980.2 17.7 %all-to-all-start = ((f32[16,6,1,2048]{3,2,1,0:T(1,128)}), f32[16,6,1,2048]{3,2,1,0:T(1,128)S(1)}, u32[]{:S(2)}, u32[]{:S(2)}) async-start(f32[16,6,1,2048]{3,2,1,0:T(1,128)} %copy.23), calls=%async_computation.2 | async-start | bytes 1572864 | tf_op jit(solution)/shard_map/all_to_all | solution.py:89
Sparse Core Ops, SparseCore 0:
  9.2 725.8 all-gather.2
  809.5 133.9 reduce-scatter.2
  946.1 31.2 reduce-scatter.4
where the time goes:
time: 1010 us
  waiting for transfers between devices  907 us (90%)
  local copies, waits for them, and re-layouts  64.2 us (6%)
  matrix products  15.9 us (2%)
  between operations  13.2 us (1%)
    all_gather x1, waiting for transfers between devices, on_device(): lax.all_gather(samples, EX_TP, axis=0, tiled=True)  728 us
    reduce_scatter x2, waiting for transfers between devices, own_block(): pieces = lax.psum_scatter(pieces, axes[k], scatter_dimension=0, tiled=True)  166 us
  transfers between devices with their start and end apart: 4, of which 4 were waited for; matrix products, arithmetic and copies ran while one was open for 0% of the time, Pallas kernels for 0%

commit v1 on v0

--- a/solution.py
+++ b/solution.py
@@ -12,6 +12,13 @@
 GATES = 44
 TP = ("tp_0", "tp_1")
 EX_TP = ("ex", "tp_0", "tp_1")
+
+
+def gather_over(block, axis, along):
+    size = lax.axis_size(axis)
+    parts = jnp.stack([block for _ in range(size)])
+    parts = lax.all_to_all(parts, axis, split_axis=0, concat_axis=0)
+    return jnp.concatenate(parts, axis=along)
 
 
 def own_block(pieces, axes, order):
@@ -73,9 +80,7 @@
     outputs = [
         jnp.maximum(
             jnp.dot(
-                lax.all_gather(samples, EX_TP, axis=0, tiled=True),
-                up_weight[0],
-                preferred_element_type=jnp.float32,
+                gather_over(samples, EX_TP, 0), up_weight[0], preferred_element_type=jnp.float32
             ),
             0.0,
         ).astype(jnp.bfloat16)

time: 1010 us -> 480 us (0.48)
  waiting for transfers between devices: 907 us -> 174 us
  blocking collectives: 0 us -> 202 us
    all_gather x1 -> x0, waiting for transfers between devices: 728 us -> none  [on_device(): lax.all_gather(samples, EX_TP, axis=0, tiled=True)]
    all_to_all x0 -> x1, blocking collectives: none -> 202 us  [gather_over(): parts = lax.all_to_all(parts, axis, split_axis=0, concat_axis=0)]
    reshape x0 -> x1, local copies, waits for them, and re-layouts: none -> 11.1 us  [gather_over(): return jnp.concatenate(parts, axis=along)]
    unnamed x21 -> x20, local copies, waits for them, and re-layouts: 11.1 us -> 0.05 us
  transfers between devices with their start and end apart: 4 -> 3, of which waited for: 4 -> 3; matrix products, arithmetic and copies ran while one was open for 0% -> 0% of each run, Pallas kernels for 0% -> 0%
where the time goes in v1:
time: 480 us; the launch traced here: 478 us
  blocking collectives  202 us (42%)
  waiting for transfers between devices  174 us (36%)
  local copies, waits for them, and re-layouts  66.1 us (14%)
  matrix products  15.9 us (3%)
  between operations  13.5 us (3%)
  starting transfers between devices  5.42 us (1%)
    all_to_all x1, blocking collectives, gather_over(): parts = lax.all_to_all(parts, axis, split_axis=0, concat_axis=0)  202 us
    reduce_scatter x2, waiting for transfers between devices, own_block(): pieces = lax.psum_scatter(pieces, axes[k], scatter_dimension=0, tiled=True)  163 us
    another operation x1, local copies, waits for them, and re-layouts, cut_along(): shard.reshape(*shape[:dim], devices, shape[dim] // devices, *shape[dim +...  19.3 us
    transpose x1, local copies, waits for them, and re-layouts, cut_along(): return jnp.moveaxis(pieces, dim, 0)  18.9 us
    dot_general x1, matrix products, on_device(): jnp.einsum('rlf,lfd->rld', hidden, down_weight, preferred_element_type=jn...  13.8 us
    all_to_all x1, waiting for transfers between devices, on_device(): lax.all_to_all(summed, 'ex', split_axis=0, concat_axis=2, tiled=True)[0]  11.6 us
    transpose x1, local copies, waits for them, and re-layouts, own_block(): pieces = pieces.transpose(*order, *range(len(axes), pieces.ndim))  11.2 us
    reshape x1, local copies, waits for them, and re-layouts, gather_over(): return jnp.concatenate(parts, axis=along)  11.1 us
  transfers between devices with their start and end apart: 3, of which 3 were waited for; matrix products, arithmetic and copies ran while one was open for 0% of the time, Pallas kernels for 0%

profile of v1, /device:TPU:1, one launch (start us, length us, event | category | flops | bytes accessed | tf_op | source)
XLA Modules:
  0.0 478.5 jit_solution(10313420806770381599)
XLA Ops:
  6.5 0.0 copy-start
  6.5 0.0 reduce-scatter.3.cloned.1.call-start
  6.5 1.9 stack.2
  8.4 202.4 %all_to_all.20 = bf16[256,6,2048]{2,1,0:T(8,128)(2,1)} all-to-all(bf16[256,6,2048]{2,1,0:T(8,128)(2,1)S(1)} %stack.2), channel_id=1, replica_groups=mesh['ex'=16,'tp_0'=2,'tp_1'=8] {'ex','tp_0','tp_1'}, dimensions={0} | all-to-all | bytes 12582912 | tf_op jit(solution)/shard_map/all_to_all | solution.py:20
  210.8 11.1 %reshape.32 = bf16[1536,2048]{1,0:T(8,128)(2,1)} reshape(bf16[256,6,2048]{2,1,0:T(8,128)(2,1)} %all_to_all.20) | data formatting | bytes 12582912 | tf_op jit(solution)/shard_map/reshape | solution.py:21
  221.9 0.0 copy-done
  221.9 0.0 copy-done.2
  222.0 13.8 %convolution_bitcast_fusion = f32[1536,1,2048]{2,0,1:T(8,128)} fusion(bf16[1,256,2048]{2,1,0:T(8,128)(2,1)S(1)} %copy-done, bf16[1536,2048]{1,0:T(8,128)(2,1)} %reshape.32, bf16[1,2048,256]{2,1,0:T(8,128)(2,1)S(1)} %copy-done.2), kind=kOutput, calls=%fused_computation | convolution fusion | flops 3222011904 | bytes 20971520 | tf_op jit(solution)/shard_map/rlf,lfd->rld/dot_general | solution.py:89
  235.7 19.3 %reshape_reshape.3 = f32[16,16,6,1,2048]{4,3,2,1,0:T(1,128)} reshape(f32[1536,1,2048]{2,0,1:T(8,128)} %convolution_bitcast_fusion) | data formatting | bytes 25165824 | tf_op jit(solution)/shard_map/reshape;reshape | solution.py:36
  255.0 18.9 %copy.21 = f32[16,16,6,1,2048]{4,1,3,2,0:T(8,128)} copy(f32[16,16,6,1,2048]{4,3,2,0,1:T(1,128)} %bitcast.39) | data formatting | bytes 25165824 | tf_op jit(solution)/shard_map/transpose | solution.py:37
  273.9 11.2 %copy.22 = f32[8,2,16,6,1,2048]{5,2,4,3,1,0:T(8,128)} copy(f32[8,2,16,6,1,2048]{5,2,4,3,0,1:T(8,128)} %bitcast.40) | data formatting | bytes 25165824 | tf_op jit(solution)/shard_map/transpose | solution.py:27
  285.1 0.0 copy-start.3
  285.1 0.0 copy-start.4
  285.1 0.0 copy-start.8
  285.1 0.0 copy-start.9
  285.1 0.0 copy-start.7
  285.1 0.0 copy-start.6
  285.2 0.0 copy-start.5
  285.2 0.0 reduce-scatter.3.cloned.1.call-update
  285.2 0.0 copy-start.1
  285.2 0.3 reduce-scatter.5.cloned.1.call-start
  285.5 130.2 %reduce-scatter.3.cloned.1.call-done = f32[2,16,6,1,2048]{4,1,3,2,0:T(8,128)} async-done(((f32[16,16,6,1,2048]{4,1,3,2,0:T(8,128)}), f32[2,16,6,1,2048]{4,1,3,2,0:T(8,128)}) %reduce-scatter.3.cloned.1.call-update) | async-done | bytes 1572880 | tf_op jit(solution)/shard_map/reduce_scatter | solution.py:30
  415.6 0.0 reduce-scatter.5.cloned.1.call-update
  415.7 0.0 copy-done.3
  415.7 0.0 copy-done.4
  415.7 0.2 fusion.29
  415.8 0.2 slice_reduce_fusion
  416.0 0.2 slice_reduce_fusion.1
  416.3 0.2 fusion.16
  416.5 0.0 copy-done.8
  416.5 0.2 fusion.10
  416.7 0.0 copy-done.9
  416.7 0.2 convolution_add_fusion.3
  416.9 32.5 %reduce-scatter.5.cloned.1.call-done = f32[1,16,6,1,2048]{4,1,3,2,0:T(8,128)} async-done(((f32[2,16,6,1,2048]{4,1,3,2,0:T(8,128)}), f32[1,16,6,1,2048]{4,1,3,2,0:T(8,128)}) %reduce-scatter.5.cloned.1.call-update) | async-done | bytes 786448 | tf_op jit(solution)/shard_map/reduce_scatter | solution.py:30
  449.4 2.8 copy.23
  452.3 5.2 %all-to-all-start.1 = ((f32[16,6,1,2048]{3,2,1,0:T(1,128)}), f32[16,6,1,2048]{3,2,1,0:T(1,128)S(1)}, u32[]{:S(2)}, u32[]{:S(2)}) async-start(f32[16,6,1,2048]{3,2,1,0:T(1,128)} %copy.23), calls=%async_computation.3 | async-start | bytes 1572864 | tf_op jit(solution)/shard_map/all_to_all | solution.py:94
  457.4 0.2 fusion.17
  457.6 0.0 copy-done.7
  457.6 0.2 convolution_add_fusion.2
  457.8 0.0 copy-done.6
  457.8 0.2 convolution_add_fusion.1
  458.0 0.0 copy-done.5
  458.0 0.2 convolution_add_fusion
  458.2 0.1 reshape.31
  458.3 11.6 %all-to-all-done.1 = f32[16,6,1,2048]{3,2,1,0:T(1,128)S(1)} async-done(((f32[16,6,1,2048]{3,2,1,0:T(1,128)}), f32[16,6,1,2048]{3,2,1,0:T(1,128)S(1)}, u32[]{:S(2)}, u32[]{:S(2)}) %all-to-all-start.1) | async-done | bytes 786464 | tf_op jit(solution)/shard_map/all_to_all | solution.py:94
  470.0 0.9 convolution_convert_fusion
  470.9 0.8 copy.25
  471.6 0.0 copy-done.1
  (1 shorter events, 0.0 us)
Async XLA Ops:
  6.5 215.4 %copy-start = (bf16[1,256,2048]{2,1,0:T(8,128)(2,1)S(1)}, bf16[1,256,2048]{2,1,0:T(8,128)(2,1)}, u32[]{:S(2)}) copy-start(bf16[1,256,2048]{2,1,0:T(8,128)(2,1)} %param.8) | copy-start | bytes 3145732
  6.5 409.1 %reduce-scatter.3.cloned.1.call-start = ((), (), s32[]{:S(2)}) async-start(), calls=%async_computation.4 | async-start | bytes 14155776 | tf_op jit(solution)/shard_map/reduce_scatter | solution.py:30
  210.8 11.1 %copy-start.2 = (bf16[1,2048,256]{2,1,0:T(8,128)(2,1)S(1)}, bf16[1,2048,256]{2,1,0:T(8,128)(2,1)}, u32[]{:S(2)}) copy-start(bf16[1,2048,256]{2,1,0:T(8,128)(2,1)} %param.7) | copy-start | bytes 3145732
  285.1 130.6 %copy-start.3 = (bf16[2048,44]{0,1:T(8,128)(2,1)S(1)}, bf16[2048,44]{0,1:T(8,128)(2,1)}, u32[]{:S(2)}) copy-start(bf16[2048,44]{0,1:T(8,128)(2,1)} %param.6) | copy-start | bytes 540676
  285.1 130.6 %copy-start.4 = (bf16[6,2048]{1,0:T(8,128)(2,1)S(1)}, bf16[6,2048]{1,0:T(8,128)(2,1)}, u32[]{:S(2)}) copy-start(bf16[6,2048]{1,0:T(8,128)(2,1)} %param.5) | copy-start | bytes 73732
  285.1 131.4 %copy-start.8 = (f32[7,80]{1,0:T(8,128)S(1)}, f32[7,80]{1,0:T(8,128)}, u32[]{:S(2)}) copy-start(f32[7,80]{1,0:T(8,128)} %constant.12) | copy-start | bytes 6724
  285.1 131.6 %copy-start.9 = (f32[7,80]{1,0:T(8,128)S(1)}, f32[7,80]{1,0:T(8,128)}, u32[]{:S(2)}) copy-start(f32[7,80]{1,0:T(8,128)} %constant.13) | copy-start | bytes 6724
  285.1 172.5 %copy-start.7 = (f32[7,80]{1,0:T(8,128)S(1)}, f32[7,80]{1,0:T(8,128)}, u32[]{:S(2)}) copy-start(f32[7,80]{1,0:T(8,128)} %constant.14) | copy-start | bytes 6724
  285.1 172.7 %copy-start.6 = (f32[7,80]{1,0:T(8,128)S(1)}, f32[7,80]{1,0:T(8,128)}, u32[]{:S(2)}) copy-start(f32[7,80]{1,0:T(8,128)} %constant.15) | copy-start | bytes 6724
  285.2 172.9 %copy-start.5 = (f32[16,80]{1,0:T(8,128)S(1)}, f32[16,80]{1,0:T(8,128)}, u32[]{:S(2)}) copy-start(f32[16,80]{1,0:T(8,128)} %constant.16) | copy-start | bytes 15364
  285.2 186.5 %copy-start.1 = (bf16[1,256,2048]{2,1,0:T(8,128)(2,1)S(1)}, bf16[1,256,2048]{2,1,0:T(8,128)(2,1)}, u32[]{:S(2)}) copy-start(bf16[1,256,2048]{2,1,0:T(8,128)(2,1)} %param.8) | copy-start | bytes 3145732
  285.2 164.2 %reduce-scatter.5.cloned.1.call-start = ((), (), s32[]{:S(2)}) async-start(), calls=%async_computation.5 | async-start | bytes 2359296 | tf_op jit(solution)/shard_map/reduce_scatter | solution.py:30
  452.3 17.7 %all-to-all-start.1 = ((f32[16,6,1,2048]{3,2,1,0:T(1,128)}), f32[16,6,1,2048]{3,2,1,0:T(1,128)S(1)}, u32[]{:S(2)}, u32[]{:S(2)}) async-start(f32[16,6,1,2048]{3,2,1,0:T(1,128)} %copy.23), calls=%async_computation.3 | async-start | bytes 1572864 | tf_op jit(solution)/shard_map/all_to_all | solution.py:94
Sparse Core Ops, SparseCore 0:
  285.3 130.2 reduce-scatter.2
  418.1 31.2 reduce-scatter.4
